TPU v7x, 32 devices: a whole 2x2x4 slice. The times are simulated.
32 devices in a mesh: col: 8 (over z, x), bin: 4 (over y, core).
Axes of the slice: x: 2, y: 2, z: 4, core: 2. Of those that a mesh axis runs over, the one named last changes fastest.
Arguments:
- slope: float32 [131072], P('bin'), may hold values from -6 to 6
- curvature: float32 [131072], P('bin'), may hold values from -6 to 0
- target_mean: float32 [131072], P('bin'), may hold values from 0.15 to 0.85
- target_var: float32 [131072], P('bin'), may hold values from 0.06 to 0.12
- table: float32 [64, 512], P(None, 'col'), may hold values from -6 to 6
Outputs:
- species_mean: float32 [64, 131072], P('col')
- final_slope: float32 [131072], replicated
All inputs are finite; a program needn't handle non-finite values.
Results may differ from a plain program's by a relative error of at most 0.0001.
Values sent between devices are 32-bit elements; how exact they have to be, the bound alone decides.
A program may use at most 64 MiB of HBM per device.

v0:
```python
import jax
import jax.numpy as jnp
from jax import lax
from jax.sharding import PartitionSpec as P

ITERS = 3


def exponent(lam, curvature, points):
    return jnp.exp(lam[None, :] * points + curvature[None, :] * points * points)


def per_device(slope, curvature, target_mean, target_var, table):
    columns = lax.axis_size("col")
    width = slope.shape[0] // columns
    offset = lax.axis_index("col") * width
    own_slope = lax.dynamic_slice_in_dim(slope, offset, width, 0)
    own_curve = lax.dynamic_slice_in_dim(curvature, offset, width, 0)
    own_mean = lax.dynamic_slice_in_dim(target_mean, offset, width, 0)
    own_var = lax.dynamic_slice_in_dim(target_var, offset, width, 0)
    full_table = lax.all_gather(table, "col", axis=1, tiled=True)
    total_pts = full_table.shape[1]
    points = ((lax.iota(jnp.int32, total_pts).astype(jnp.float32) + 0.5) / total_pts)[:, None]
    own_lam = own_slope
    for step in range(ITERS):
        expo = exponent(own_lam, own_curve, points)
        partition = jnp.sum(expo, axis=0)
        moment = jnp.sum(points * expo, axis=0)
        own_lam = own_lam + (own_mean - moment / partition) / own_var
    expo = exponent(own_lam, own_curve, points)
    weights = expo / jnp.sum(expo, axis=0)[None, :]
    terms = jnp.dot(
        full_table, weights, precision=lax.Precision.HIGHEST, preferred_element_type=jnp.float32
    )
    species = lax.all_to_all(terms, "col", split_axis=0, concat_axis=1, tiled=True)
    lam = lax.all_gather(own_lam, "col", axis=0, tiled=True)
    species_mean, final_slope = (
        lax.all_gather(species, "bin", axis=1, tiled=True),
        lax.all_gather(lam, "bin", axis=0, tiled=True),
    )
    return (species_mean, final_slope)


def solution(mesh):
    placed = (P("bin"), P("bin"), P("bin"), P("bin"), P(None, "col"))
    return jax.shard_map(
        per_device, mesh=mesh, in_specs=placed, out_specs=(P("col", None), P()), check_vma=False
    )
```

profile of v0, /device:TPU:0, one launch (start us, length us, event | category | flops | bytes accessed | tf_op | source)
XLA Modules:
  0.0 136.4 jit_solution(17410664243535203847)
XLA Ops:
  7.2 0.0 all-gather.2.cloned.1.call-start
  7.2 0.7 dynamic_slice.14
  8.0 0.7 dynamic_slice.12
  8.7 2.7 %fusion.4 = (f32[4096]{0:T(1024)S(1)}, f32[4096]{0:T(1024)S(1)}) fusion(f32[4096]{0:T(1024)S(1)} %dynamic_slice.14, f32[4096]{0:T(1024)S(1)} %dynamic_slice.12, f32[512]{0:T(512)S(1)} %add_multiply_fusion), kind=kLoop, calls=%fused_computation.12 | loop fusion | flops 14671872 | bytes 67584 | tf_op jit(solution)/shard_map/reduce_sum | solution.py:27
  11.4 0.8 divide_add_fusion.2
  12.2 2.7 %fusion = (f32[4096]{0:T(1024)S(1)}, f32[4096]{0:T(1024)S(1)}) fusion(f32[4096]{0:T(1024)S(1)} %divide_add_fusion.2, f32[4096]{0:T(1024)S(1)} %dynamic_slice.14, f32[512]{0:T(512)S(1)} %add_multiply_fusion), kind=kLoop, calls=%fused_computation.8 | loop fusion | flops 14671872 | bytes 67584 | tf_op jit(solution)/shard_map/reduce_sum | solution.py:27
  14.9 0.0 copy-start
  14.9 0.8 divide_add_fusion.1
  15.6 2.7 %fusion.1 = (f32[4096]{0:T(1024)S(1)}, f32[4096]{0:T(1024)S(1)}) fusion(f32[4096]{0:T(1024)S(1)} %divide_add_fusion.1, f32[4096]{0:T(1024)S(1)} %dynamic_slice.14, f32[512]{0:T(512)S(1)} %add_multiply_fusion), kind=kLoop, calls=%fused_computation.9 | loop fusion | flops 14671872 | bytes 67584 | tf_op jit(solution)/shard_map/reduce_sum | solution.py:27
  18.4 0.8 divide_add_fusion
  19.1 2.1 %fusion.3 = f32[4096]{0:T(1024)S(1)} fusion(f32[4096]{0:T(1024)S(1)} %divide_add_fusion, f32[4096]{0:T(1024)S(1)} %dynamic_slice.14, f32[512]{0:T(512)S(1)} %add_multiply_fusion), kind=kLoop, calls=%fused_computation.11 | loop fusion | flops 10481664 | bytes 51200 | tf_op jit(solution)/shard_map/reduce_sum | solution.py:31
  21.3 0.0 copy-done
  21.3 0.1 copy.8
  21.3 32.7 %all_gather.12 = f32[64,512]{0,1:T(8,128)S(1)} all-gather(f32[64,64]{0,1:T(8,128)S(1)} %copy.8), channel_id=1, replica_groups=mesh['col'=8,'bin'=4] {'col'}, dimensions={1}, use_global_device_ids=true | all-gather | bytes 147456 | tf_op jit(solution)/shard_map/all_gather | solution.py:21
  54.1 7.4 %fusion.7 = f32[8,8,4096]{2,1,0:T(8,128)S(1)} fusion(f32[64,512]{0,1:T(8,128)S(1)} %all_gather.12, f32[4096]{0:T(1024)S(1)} %fusion.3, f32[4096]{0:T(1024)S(1)} %divide_add_fusion, f32[4096]{0:T(1024)S(1)} %dynamic_slice.14, f32[512]{0:T(512)S(1)} %add_multiply_fusion), kind=kOutput, calls=%fused_computation.14 | convolution fusion | flops 1621098496 | bytes 1230848 | tf_op jit(solution)/shard_map/dot_general | solution.py:32
  61.5 25.0 %all_to_all.19 = f32[8,8,4096]{2,1,0:T(8,128)} all-to-all(f32[8,8,4096]{2,1,0:T(8,128)S(1)} %fusion.7), channel_id=1, replica_groups=mesh['col'=8,'bin'=4] {'col'}, dimensions={0} | all-to-all | bytes 2097152 | tf_op jit(solution)/shard_map/all_to_all | solution.py:35
  86.5 0.0 all-gather.2.cloned.1.call-update
  86.5 30.5 %all_gather.14 = f32[32768]{0:T(1024)S(1)} all-gather(f32[4096]{0:T(1024)S(1)} %divide_add_fusion), channel_id=1, replica_groups=mesh['col'=8,'bin'=4] {'col'}, dimensions={0}, use_global_device_ids=true | all-gather | bytes 147456 | tf_op jit(solution)/shard_map/all_gather | solution.py:36
  117.0 7.2 %all_gather.15 = f32[131072]{0:T(1024)S(1)} all-gather(f32[32768]{0:T(1024)S(1)} %all_gather.14), channel_id=1, replica_groups=mesh['col'=8,'bin'=4] {'bin'}, dimensions={0}, use_global_device_ids=true | all-gather | bytes 655360 | tf_op jit(solution)/shard_map/all_gather | solution.py:39
  124.2 0.0 all-gather.2.cloned.1.call-done
  124.2 4.5 %copy.11 = f32[8,131072]{1,0:T(8,128)} copy(f32[8,131072]{1,0:T(8,128)} %all-gather.2.cloned.1.call-done) | data formatting | bytes 8388608
  128.7 0.8 copy.12
  (1 shorter events, 0.0 us)
Async XLA Ops:
  7.2 117.1 %all-gather.2.cloned.1.call-start = ((), (), s32[]{:S(2)}) async-start(), calls=%async_computation.1 | async-start | bytes 5242880 | tf_op jit(solution)/shard_map/all_gather | solution.py:38
  14.9 6.4 %copy-start = (f32[64,64]{1,0:T(8,128)S(1)}, f32[64,64]{1,0:T(8,128)}, u32[]{:S(2)}) copy-start(f32[64,64]{1,0:T(8,128)} %param.9) | copy-start | bytes 49156
Sparse Core Ops, SparseCore 0:
  86.6 33.3 all-gather.1
where the time goes:
time: 137 us; the launch traced here: 136 us
  blocking collectives  95.4 us (70%)
  between operations  14.1 us (10%)
  other arithmetic  12.6 us (9%)
  matrix products  7.4 us (5%)
  local copies, waits for them, and re-layouts  6.82 us (5%)
    all_gather x1, blocking collectives, per_device(): full_table = lax.all_gather(table, 'col', axis=1, tiled=True)  32.7 us
    all_gather x1, blocking collectives, per_device(): lam = lax.all_gather(own_lam, 'col', axis=0, tiled=True)  30.5 us
    all_to_all x1, blocking collectives, per_device(): lax.all_to_all(terms, 'col', split_axis=0, concat_axis=1, tiled=True)  25 us
    reduce_sum x3, other arithmetic, per_device(): partition = jnp.sum(expo, axis=0)  8.13 us
    dot_general x1, matrix products, per_device(): jnp.dot(full_table, weights, precision=lax.Precision.HIGHEST, preferred_e...  7.4 us
    all_gather x1, blocking collectives, per_device(): lax.all_gather(lam, 'bin', axis=0, tiled=True)  7.18 us
    unnamed x5, local copies, waits for them, and re-layouts  5.38 us
  transfers between devices with their start and end apart: 1, of which 0 were waited for; matrix products, arithmetic and copies ran while one was open for 0% of the time, Pallas kernels for 0%

commit v1 on v0

v1 whole, which is shorter than its diff:
```python
import functools
import math
import jax
import jax.numpy as jnp
from jax import lax
from jax.experimental import pallas as pl
from jax.experimental.pallas import tpu as pltpu
from jax.sharding import PartitionSpec as P

ITERS = 3
LANES = 128
LOG2E = math.log2(math.e)
MESH = pl.DeviceIdType.MESH
GROUP = 16


def kernel(
    cols, bins, total_pts, rows,
    slope_ref, curve_ref, mean_ref, var_ref, placed_ref,
    out_ref, lam_ref,
    tab, lhs, species,
    bar_unused, tsend, trecv, csend, crecv, ssend, srecv, lsend, lrecv, osem,
):
    del bar_unused
    col = lax.axis_index("col")
    me = lax.axis_index("bin")
    core = lax.rem(me, 2)
    partner = me + 1 - 2 * core
    chips = bins // 2
    width = slope_ref.shape[1] * LANES

    def other_col(i):
        return lax.rem(col + i, cols)

    def other_chip(i):
        return lax.rem(me + 2 * i, bins)

    barrier = pltpu.get_barrier_semaphore()

    @pl.loop(1, cols)
    def _(i):
        pl.semaphore_signal(barrier, inc=1, device_id=(other_col(i), me), device_id_type=MESH)

    for i in range(1, chips):
        pl.semaphore_signal(barrier, inc=1, device_id=(col, other_chip(i)), device_id_type=MESH)
    pl.semaphore_signal(barrier, inc=1, device_id=(col, partner), device_id_type=MESH)

    curve2 = curve_ref[col] * LOG2E
    target = mean_ref[col]
    var = var_ref[col]
    lam = slope_ref[col]

    def newton(lam):
        lam2 = lam * LOG2E

        def body(g, carry):
            part, mom = carry
            for i in range(GROUP):
                c = ((g * GROUP + i).astype(jnp.float32) + 0.5) * (1.0 / total_pts)
                e = jnp.exp2(c * (lam2 + curve2 * c))
                part = part + e
                mom = mom + c * e
            return part, mom

        zero = jnp.zeros_like(lam)
        part, mom = lax.fori_loop(0, total_pts // GROUP, body, (zero, zero))
        return lam + (target - mom / part) / var

    lam = newton(lam)

    pl.semaphore_wait(barrier, cols - 1 + chips)

    def table_copy(i):
        to = other_col(i)
        return pltpu.make_async_remote_copy(
            src_ref=placed_ref.at[to], dst_ref=tab.at[i],
            send_sem=tsend.at[i], recv_sem=trecv.at[i],
            device_id=(to, me), device_id_type=MESH,
        )

    @pl.loop(1, cols)
    def _(i):
        table_copy(i).start()

    for step in range(1, ITERS):
        lam = newton(lam)
    lam_ref[me, col] = lam

    def lam_copy(i):
        to = other_col(i)
        return pltpu.make_async_remote_copy(
            src_ref=lam_ref.at[me, col], dst_ref=lam_ref.at[me, col],
            send_sem=csend.at[i], recv_sem=crecv.at[cols - i],
            device_id=(to, me), device_id_type=MESH,
        )

    def lam_arrival(s):
        src = other_col(s)
        return pltpu.make_async_remote_copy(
            src_ref=lam_ref.at[me, src], dst_ref=lam_ref.at[me, src],
            send_sem=csend.at[s], recv_sem=crecv.at[s],
            device_id=(src, me), device_id_type=MESH,
        )

    @pl.loop(1, cols)
    def _(i):
        lam_copy(i).start()

    @pl.loop(1, cols)
    def _(i):
        table_copy(i).wait()

    full = placed_ref[col]
    full = lax.fori_loop(1, cols, lambda i, acc: acc + tab[i], full)
    high = full.astype(jnp.bfloat16).astype(jnp.float32)
    low = full - high
    pad = full.shape[0]
    ones = jnp.ones((pad, total_pts), jnp.float32)
    lhs[...] = jnp.concatenate([high, low, ones, jnp.zeros_like(ones)], axis=0).astype(jnp.bfloat16)

    def species_copy(n, b, j, dest):
        return pltpu.make_async_remote_copy(
            src_ref=species.at[b, j], dst_ref=species.at[b, j],
            send_sem=ssend.at[n, j], recv_sem=srecv.at[b, j],
            device_id=(col, dest), device_id_type=MESH,
        )

    def slope_copy(n, b, j, dest):
        return pltpu.make_async_remote_copy(
            src_ref=lam_ref.at[b, j], dst_ref=lam_ref.at[b, j],
            send_sem=lsend.at[n, j], recv_sem=lrecv.at[b, j],
            device_id=(col, dest), device_id_type=MESH,
        )

    def write_out(b, j):
        start = pl.multiple_of((b * cols + j) * width, LANES)
        return pltpu.make_async_copy(
            species.at[b, j], out_ref.at[:, pl.ds(start, width)], osem.at[b, j]
        )

    half = min(256, total_pts)

    def compute(j):
        @pl.loop(0, width // (2 * LANES))
        def _(t):
            r = t * 2
            lam_t = jnp.concatenate([lam_ref[me, j, pl.ds(r, 1)], lam_ref[me, j, pl.ds(r + 1, 1)]], axis=1) * LOG2E
            cur_t = jnp.concatenate([curve_ref[j, pl.ds(r, 1)], curve_ref[j, pl.ds(r + 1, 1)]], axis=1) * LOG2E
            acc_h = jnp.zeros((4 * pad, 2 * LANES), jnp.float32)
            for k in range(total_pts // half):
                c = (lax.broadcasted_iota(jnp.int32, (half, 2 * LANES), 0).astype(jnp.float32)
                     + (k * half + 0.5)) * (1.0 / total_pts)
                e = jnp.exp2(c * (lam_t + cur_t * c))
                e_hi = e.astype(jnp.bfloat16)
                e_lo = (e - e_hi.astype(jnp.float32)).astype(jnp.bfloat16)
                w = lhs[:, k * half:(k + 1) * half]
                acc_h = acc_h + jnp.dot(w, e_hi, preferred_element_type=jnp.float32)
                acc_h = acc_h + jnp.dot(w, e_lo, preferred_element_type=jnp.float32)
            total = acc_h[2 * pad:3 * pad]
            value = (acc_h[:pad] + acc_h[pad:2 * pad]) / total
            at = pl.multiple_of(t * 2 * LANES, 2 * LANES)
            species[me, j, :, pl.ds(at, 2 * LANES)] = value[:rows]

    def relay(j):
        for i in range(1, chips):
            b = other_chip(i)
            species_copy(chips + i - 1, b, j, partner).wait_recv()
            species_copy(chips + i - 1, b, j, partner).start()
            write_out(b, j).start()
            slope_copy(chips + i - 1, b, j, partner).wait_recv()
            slope_copy(chips + i - 1, b, j, partner).start()

    def send_own(j):
        for i in range(1, chips):
            species_copy(i, me, j, other_chip(i)).start()
            slope_copy(i, me, j, other_chip(i)).start()
        species_copy(0, me, j, partner).start()
        slope_copy(0, me, j, partner).start()
        write_out(me, j).start()

    @pl.loop(0, cols)
    def _(s):
        j = other_col(s)

        @pl.when(s > 0)
        def _():
            lam_arrival(s).wait_recv()

        compute(j)
        send_own(j)

        @pl.when(s > 1)
        def _():
            relay(other_col(s + cols - 2))

    for s in range(max(cols - 2, 0), cols):
        relay(other_col(s))

    @pl.loop(0, cols)
    def _(s):
        j = other_col(s)
        for i in range(chips):
            b = lax.rem(partner + 2 * i, bins)
            species_copy(0, b, j, partner).wait_recv()
            slope_copy(0, b, j, partner).wait_recv()
            write_out(b, j).start()

    @pl.loop(0, cols)
    def _(s):
        j = other_col(s)
        for n in range(2 * chips - 1):
            species_copy(n, me, j, partner).wait_send()
            slope_copy(n, me, j, partner).wait_send()
        for b in range(bins):
            write_out(b, j).wait()

    @pl.loop(1, cols)
    def _(i):
        lam_copy(i).wait_send()


def per_device(slope, curvature, target_mean, target_var, table):
    cols = lax.axis_size("col")
    bins = lax.axis_size("bin")
    all_species, pts = table.shape
    rows = all_species // cols
    pad = -(-rows // 8) * 8
    total_pts = pts * cols
    per_shard = slope.shape[0]
    sub = per_shard // cols // LANES
    width = sub * LANES

    def blocks(a):
        return a.reshape(cols, sub, LANES)

    placed = jnp.zeros((cols, pad, total_pts), jnp.float32)
    placed = lax.dynamic_update_slice(
        placed, table.reshape(cols, rows, pts), (0, 0, lax.axis_index("col") * pts)
    )
    vmem = pl.BlockSpec(memory_space=pltpu.VMEM)
    chips = bins // 2
    dma = pltpu.SemaphoreType.DMA
    species_mean, lam = pl.pallas_call(
        functools.partial(kernel, cols, bins, total_pts, rows),
        out_shape=(
            jax.ShapeDtypeStruct((rows, per_shard * bins), jnp.float32),
            jax.ShapeDtypeStruct((bins, cols, sub, LANES), jnp.float32),
        ),
        in_specs=[vmem] * 5,
        out_specs=(pl.BlockSpec(memory_space=pl.ANY), vmem),
        scratch_shapes=[
            pltpu.VMEM((cols, pad, total_pts), jnp.float32),
            pltpu.VMEM((4 * pad, total_pts), jnp.bfloat16),
            pltpu.VMEM((bins, cols, rows, width), jnp.float32),
            pltpu.SMEM((1,), jnp.int32),
            dma((cols,)), dma((cols,)),
            dma((cols,)), dma((cols,)),
            dma((2 * chips - 1, cols)), dma((bins, cols)),
            dma((2 * chips - 1, cols)), dma((bins, cols)),
            dma((bins, cols)),
        ],
        compiler_params=pltpu.CompilerParams(collective_id=0, has_side_effects=True, vmem_limit_bytes=48 << 20),
    )(blocks(slope), blocks(curvature), blocks(target_mean), blocks(target_var), placed)
    return species_mean, lam.reshape(-1)


def solution(mesh):
    placed = (P("bin"), P("bin"), P("bin"), P("bin"), P(None, "col"))
    return jax.shard_map(
        per_device, mesh=mesh, in_specs=placed, out_specs=(P("col", None), P()), check_vma=False
    )
```

time: 137 us -> 70.7 us (0.52)
  blocking collectives: 95.4 us -> 0 us
  Pallas kernels: 0 us -> 62.4 us
  between operations: 14.1 us -> 0.67 us
  other arithmetic: 12.6 us -> 0 us
  matrix products: 7.4 us -> 0 us
    all_gather x3 -> x0, blocking collectives: 70.4 us -> none  [the longest x1 32.7 us: per_device(): full_table = lax.all_gather(table, 'col', axis=1, tiled=True)]
    pallas_call x0 -> x1, Pallas kernels: none -> 62.4 us  [per_device(): pl.pallas_call(functools.partial(kernel, cols, bins, total_pts, rows), ou...]
    all_to_all x1 -> x0, blocking collectives: 25 us -> none  [per_device(): lax.all_to_all(terms, 'col', split_axis=0, concat_axis=1, tiled=True)]
    reduce_sum x4 -> x0, other arithmetic: 10.3 us -> none  [the longest x3 8.13 us: per_device(): partition = jnp.sum(expo, axis=0)]
    dot_general x1 -> x0, matrix products: 7.4 us -> none  [per_device(): jnp.dot(full_table, weights, precision=lax.Precision.HIGHEST, preferred_e...]
    add x3 -> x0, other arithmetic: 2.29 us -> none  [per_device(): own_lam = own_lam + (own_mean - moment / partition) / own_var]
    dynamic_slice x2 -> x0, local copies, waits for them, and re-layouts: 1.44 us -> none  [the longest x1 0.72 us: per_device(): own_curve = lax.dynamic_slice_in_dim(curvature, offset, width, 0)]
    unnamed x5 -> x10, local copies, waits for them, and re-layouts: 5.38 us -> 6.45 us
  transfers between devices with their start and end apart: 1 -> 0, of which waited for: 0 -> 0; matrix products, arithmetic and copies ran while one was open for 0% -> 0% of each run, Pallas kernels for 0% -> 0%
where the time goes in v1:
time: 70.7 us; the launch traced here: 70.4 us
  Pallas kernels  62.4 us (88%)
  local copies, waits for them, and re-layouts  7.37 us (10%)
    pallas_call x1, Pallas kernels, per_device(): pl.pallas_call(functools.partial(kernel, cols, bins, total_pts, rows), ou...  62.4 us
    unnamed x10, local copies, waits for them, and re-layouts  6.45 us

profile of v1, /device:TPU:0, one launch (start us, length us, event | category | flops | bytes accessed | tf_op | source)
XLA Modules:
  0.0 70.4 jit_solution(18100505404065436393)
XLA Ops:
  0.7 0.9 %dynamic_update_slice.3.placed_ref = f32[8,8,512]{2,1,0:T(8,128)S(1)} dynamic-update-slice(f32[8,8,512]{2,1,0:T(8,128)S(1)} %broadcast_in_dim.3, f32[8,8,64]{2,1,0:T(8,128)} %bitcast.11, s32[]{:T(128)} %constant.3.clone.1, s32[]{:T(128)} %constant.3.clone.1, s32[]{:T(128)S(6)} %select_n.3) | dynamic-update-slice | bytes 32772 | tf_op jit(solution)/shard_map/dynamic_update_slice | solution.py:237
  1.6 0.0 copy-start
  1.6 0.9 %copy-done = f32[32768]{0:T(1024)S(1)} copy-done((f32[32768]{0:T(1024)S(1)}, f32[32768]{0:T(1024)}, u32[]{:S(2)}) %copy-start) | copy-done | bytes 131096
  2.5 0.0 copy-start.1
  2.5 0.9 %copy-done.1 = f32[32768]{0:T(1024)S(1)} copy-done((f32[32768]{0:T(1024)S(1)}, f32[32768]{0:T(1024)}, u32[]{:S(2)}) %copy-start.1) | copy-done | bytes 131096
  3.4 0.0 copy-start.2
  3.4 0.9 %copy-done.2 = f32[32768]{0:T(1024)S(1)} copy-done((f32[32768]{0:T(1024)S(1)}, f32[32768]{0:T(1024)}, u32[]{:S(2)}) %copy-start.2) | copy-done | bytes 131096
  4.3 0.0 copy-start.3
  4.3 0.9 %copy-done.3 = f32[32768]{0:T(1024)S(1)} copy-done((f32[32768]{0:T(1024)S(1)}, f32[32768]{0:T(1024)}, u32[]{:S(2)}) %copy-start.3) | copy-done | bytes 131096
  5.2 62.4 %shard_map.68 = (f32[8,131072]{1,0:T(8,128)S(1)}, f32[4,8,32,128]{3,2,1,0:T(8,128)S(1)}) custom-call(f32[8,32,128]{2,1,0:T(8,128)S(1)} %bitcast.7, f32[8,32,128]{2,1,0:T(8,128)S(1)} %bitcast.8, f32[8,32,128]{2,1,0:T(8,128)S(1)} %bitcast.9, f32[8,32,128]{2,1,0:T(8,128)S(1)} %bitcast.10, f32[8,8,512]{2,1,0:T(8,128)S(1)} %dynamic_update_slice.3.placed_ref), custom_call_target="tpu_custom_call" | custom-call | tf_op jit(solution)/shard_map/pallas_call | solution.py:243
  67.6 2.0 %copy.10 = f32[8,131072]{1,0:T(8,128)} copy(f32[8,131072]{1,0:T(8,128)S(1)} %get-tuple-element.8) | data formatting | bytes 8388608
  69.6 0.8 %copy.11 = f32[131072]{0:T(1024)} copy(f32[131072]{0:T(1024)S(1)} %bitcast.6) | data formatting | bytes 1048576
  (1 shorter events, 0.0 us)
Async XLA Ops:
  1.6 0.9 %copy-start = (f32[32768]{0:T(1024)S(1)}, f32[32768]{0:T(1024)}, u32[]{:S(2)}) copy-start(f32[32768]{0:T(1024)} %param.5) | copy-start | bytes 393220
  2.5 0.9 %copy-start.1 = (f32[32768]{0:T(1024)S(1)}, f32[32768]{0:T(1024)}, u32[]{:S(2)}) copy-start(f32[32768]{0:T(1024)} %param.6) | copy-start | bytes 393220
  3.4 0.9 %copy-start.2 = (f32[32768]{0:T(1024)S(1)}, f32[32768]{0:T(1024)}, u32[]{:S(2)}) copy-start(f32[32768]{0:T(1024)} %param.7) | copy-start | bytes 393220
  4.3 0.9 %copy-start.3 = (f32[32768]{0:T(1024)S(1)}, f32[32768]{0:T(1024)}, u32[]{:S(2)}) copy-start(f32[32768]{0:T(1024)} %param.8) | copy-start | bytes 393220

commit v2 on v0

v2 whole, which is shorter than its diff:
```python
import functools
import math
import jax
import jax.numpy as jnp
from jax import lax
from jax.experimental import pallas as pl
from jax.experimental.pallas import tpu as pltpu
from jax.sharding import PartitionSpec as P

ITERS = 3
LANES = 128
LOG2E = math.log2(math.e)
MESH = pl.DeviceIdType.MESH
UNROLL = 16
GROUP = 4
PARTS = 4


def kernel(
    cols, bins, total_pts, rows,
    slope_hbm, curve_hbm, mean_hbm, var_hbm, placed_ref,
    out_ref, lam_ref,
    own, curve, tab, lhs, points, stage, species,
    isem, tsend, trecv, ksend, krecv, asend, arecv, bsend, brecv, lsend, lrecv,
    msend, mrecv, ysend, yrecv, psend, precv, osem,
):
    col = lax.axis_index("col")
    me = lax.axis_index("bin")
    core = lax.rem(me, 2)
    partner = me + 1 - 2 * core
    chips = bins // 2
    groups = cols // GROUP
    member = lax.rem(col, GROUP)
    group = col // GROUP
    sub = own.shape[1]
    width = sub * LANES
    part = width // PARTS
    part_rows = sub // PARTS
    pad = placed_ref.shape[1]

    def other_chip(i):
        return lax.rem(me + 2 * i, bins)

    def peer(u, d):
        return lax.rem(group + u, groups) * GROUP + lax.rem(member + d, GROUP)

    def remote(src, dst, send, recv, c, b):
        return pltpu.make_async_remote_copy(
            src_ref=src, dst_ref=dst, send_sem=send, recv_sem=recv,
            device_id=(c, b), device_id_type=MESH,
        )

    barrier = pltpu.get_barrier_semaphore()

    @pl.loop(1, cols)
    def _(i):
        pl.semaphore_signal(barrier, inc=1, device_id=(lax.rem(col + i, cols), me), device_id_type=MESH)

    for i in range(1, chips):
        @pl.loop(0, groups)
        def _(u):
            pl.semaphore_signal(barrier, inc=1, device_id=(peer(u, 0), other_chip(i)), device_id_type=MESH)

    pl.semaphore_signal(barrier, inc=1, device_id=(col, partner), device_id_type=MESH)

    loads = [
        pltpu.make_async_copy(a.at[col], own.at[n], isem.at[n])
        for n, a in enumerate((slope_hbm, mean_hbm, var_hbm))
    ]
    loads.append(pltpu.make_async_copy(curve_hbm, curve.at[me], isem.at[3]))
    for load in loads:
        load.start()
    tab[col] = placed_ref[pl.ds(group * GROUP, GROUP)]
    points[...] = (lax.broadcasted_iota(jnp.int32, points.shape, 0).astype(jnp.float32) + 0.5) * (1.0 / total_pts)
    for load in loads:
        load.wait()

    curve2 = curve[me, col] * LOG2E
    target = own[1]
    var = own[2]
    lam = own[0]

    def newton(lam):
        lam2 = lam * LOG2E

        def body(g, carry):
            total, mom = carry
            for i in range(UNROLL):
                c = ((g * UNROLL + i).astype(jnp.float32) + 0.5) * (1.0 / total_pts)
                e = jnp.exp2(c * (lam2 + curve2 * c))
                total = total + e
                mom = mom + c * e
            return total, mom

        zero = jnp.zeros_like(lam)
        total, mom = lax.fori_loop(0, total_pts // UNROLL, body, (zero, zero))
        return lam + (target - mom / total) / var

    lam = newton(lam)
    pl.semaphore_wait(barrier, cols - 1 + (chips - 1) * groups + 1)

    def table_copy(i):
        to = lax.rem(col + i, cols)
        return remote(placed_ref.at[pl.ds(to // GROUP * GROUP, GROUP)], tab.at[col], tsend.at[i], trecv.at[col], to, me)

    def table_arrival(i):
        src = lax.rem(col + i, cols)
        return remote(tab.at[src], tab.at[src], tsend.at[i], trecv.at[src], src, me)

    def curve_copy(i, u):
        j = peer(u, 0)
        to = other_chip(i)
        return remote(curve.at[me, j], curve.at[me, j], ksend.at[i, u], krecv.at[me // 2, j], col, to)

    def curve_arrival(i, u):
        j = peer(u, 0)
        b = other_chip(i)
        return remote(curve.at[b, j], curve.at[b, j], ksend.at[i, u], krecv.at[b // 2, j], col, b)

    @pl.loop(1, cols)
    def _(i):
        table_copy(i).start()

    for i in range(1, chips):
        @pl.loop(0, groups)
        def _(u):
            curve_copy(i, u).start()

    for step in range(1, ITERS):
        lam = newton(lam)
    lam_ref[me, col] = lam

    def first_copy(i, u):
        return remote(lam_ref.at[me, col], lam_ref.at[me, col], asend.at[i, u], arecv.at[me // 2, col], peer(u, 0), other_chip(i))

    def first_arrival(i, u):
        j = peer(u, 0)
        b = other_chip(i)
        return remote(lam_ref.at[b, j], lam_ref.at[b, j], asend.at[i, u], arecv.at[b // 2, j], j, b)

    @pl.loop(1, groups)
    def _(u):
        first_copy(0, u).start()

    for i in range(1, chips):
        @pl.loop(0, groups)
        def _(u):
            first_copy(i, u).start()

    @pl.loop(1, cols)
    def _(i):
        table_arrival(i).wait_recv()

    per = LANES // (total_pts // cols)
    tiles = []
    for t in range(total_pts // LANES):
        block = tab[t * per]
        for n in range(1, per):
            block = block + tab[t * per + n]
        tiles.append(block.reshape(GROUP * pad, LANES))
    full = jnp.concatenate(tiles, axis=1)
    high = full.astype(jnp.bfloat16).astype(jnp.float32)
    ones = jnp.ones((16, total_pts), jnp.float32)
    lhs[...] = jnp.concatenate([high, full - high, ones], axis=0).astype(jnp.bfloat16)

    span = GROUP * pad

    def lanes(q):
        return pl.ds(pl.multiple_of(q * part, LANES), part)

    def compute(item, b, j, q):
        @pl.loop(0, part_rows // 2)
        def _(t):
            highs, lows = [], []
            for n in range(2):
                r = q * part_rows + t * 2 + n
                lam_t = lam_ref[b, j, pl.ds(r, 1)] * LOG2E
                cur_t = curve[b, j, pl.ds(r, 1)] * LOG2E
                c = points[...]
                e = jnp.exp2(c * (lam_t + cur_t * c))
                e_hi = e.astype(jnp.bfloat16)
                highs.append(e_hi)
                lows.append((e - e_hi.astype(jnp.float32)).astype(jnp.bfloat16))
            acc = jnp.dot(lhs[...], jnp.concatenate(highs, axis=1), preferred_element_type=jnp.float32)
            acc = acc + jnp.dot(lhs[...], jnp.concatenate(lows, axis=1), preferred_element_type=jnp.float32)
            value = (acc[:span] + acc[span:2 * span]) / acc[2 * span:2 * span + 1]
            at = pl.ds(pl.multiple_of(t * 2 * LANES, 2 * LANES), 2 * LANES)
            for n in range(GROUP):
                stage[item, n, :, at] = value[n * pad:n * pad + rows]
            into = pl.ds(pl.multiple_of(q * part + t * 2 * LANES, 2 * LANES), 2 * LANES)
            species[b, j, :, into] = stage[item, member, :, at]

    def member_copy(item, d, b, j, q):
        to = lax.rem(member + d, GROUP)
        return remote(stage.at[item, to], species.at[b, j, :, lanes(q)], msend.at[item, d], mrecv.at[b // 2, j, q], group * GROUP + to, me)

    def member_arrival(b, j, q):
        return remote(species.at[b, j, :, lanes(q)], species.at[b, j, :, lanes(q)], msend.at[0, 0], mrecv.at[b // 2, j, q], lax.rem(col + 1, cols), me)

    def y_copy(i, j, q):
        at = species.at[me, j, :, lanes(q)]
        return remote(at, at, ysend.at[i, j, q], yrecv.at[me // 2, j, q], col, other_chip(i))

    def y_arrival(i, j, q):
        b = other_chip(i)
        at = species.at[b, j, :, lanes(q)]
        return remote(at, at, ysend.at[i, j, q], yrecv.at[b // 2, j, q], col, b)

    def pair_copy(b, j, q):
        at = species.at[b, j, :, lanes(q)]
        return remote(at, at, psend.at[b // 2, j], precv.at[b // 2, j], col, partner)

    def pair_chunk(b, j):
        at = species.at[b, j]
        return remote(at, at, psend.at[b // 2, j], precv.at[b // 2, j], col, partner)

    def write_part(b, j, q):
        start = pl.multiple_of((b * cols + j) * width + q * part, LANES)
        return pltpu.make_async_copy(species.at[b, j, :, lanes(q)], out_ref.at[:, pl.ds(start, part)], osem.at[b, j])

    def write_chunk(b, j):
        start = pl.multiple_of((b * cols + j) * width, LANES)
        return pltpu.make_async_copy(species.at[b, j], out_ref.at[:, pl.ds(start, width)], osem.at[b, j])

    def hand_on(b, j, q):
        pair_copy(b, j, q).start()
        write_part(b, j, q).start()

    singles = groups * (PARTS - 1)

    def single(s):
        return s // (PARTS - 1), 1 + lax.rem(s, PARTS - 1)

    def single_arrivals(s):
        u, q = single(s)
        for d in range(1, GROUP):
            j = peer(u, d)
            member_arrival(me, j, q).wait_recv()
            for i in range(1, chips):
                y_copy(i, j, q).start()
            hand_on(me, j, q)

    @pl.loop(0, singles)
    def _(s):
        u, q = single(s)
        j = peer(u, 0)

        @pl.when(jnp.logical_and(q == 1, u > 0))
        def _():
            first_arrival(0, u).wait_recv()

        compute(s, me, j, q)
        for i in range(1, chips):
            y_copy(i, j, q).start()
        for d in range(1, GROUP):
            member_copy(s, d, me, j, q).start()
        hand_on(me, j, q)

        @pl.when(s > 1)
        def _():
            single_arrivals(s - 2)

    for i in range(1, chips):
        @pl.loop(0, groups)
        def _(u):
            first_arrival(i, u).wait_recv()
            curve_arrival(i, u).wait_recv()

    doubles = groups * chips

    @pl.loop(0, doubles)
    def _(s):
        u = s // chips
        b = lax.rem(me + 2 * lax.rem(s, chips), bins)
        j = peer(u, 0)
        compute(singles + s, b, j, 0)
        for d in range(1, GROUP):
            member_copy(singles + s, d, b, j, 0).start()
        hand_on(b, j, 0)

        @pl.when(s < 2)
        def _():
            single_arrivals(singles - 2 + s)

    def second_copy(d, b, j):
        to = lax.rem(member + d, GROUP)
        return remote(lam_ref.at[b, j], lam_ref.at[b, j], bsend.at[b // 2, j // GROUP, d], brecv.at[b // 2, j], group * GROUP + to, me)

    @pl.loop(0, doubles)
    def _(s):
        b = lax.rem(me + 2 * lax.rem(s, chips), bins)
        for d in range(1, GROUP):
            second_copy(d, b, peer(s // chips, 0)).start()

    @pl.loop(0, doubles)
    def _(s):
        b = lax.rem(me + 2 * lax.rem(s, chips), bins)
        for d in range(1, GROUP):
            j = peer(s // chips, d)
            member_arrival(b, j, 0).wait_recv()
            hand_on(b, j, 0)

    @pl.loop(0, singles)
    def _(s):
        u, q = single(s)
        for d in range(GROUP):
            for i in range(1, chips):
                y_arrival(i, peer(u, d), q).wait_recv()
                hand_on(other_chip(i), peer(u, d), q)

    def lam_pair(b):
        return remote(lam_ref.at[b], lam_ref.at[b], lsend.at[b // 2], lrecv.at[b // 2], col, partner)

    for i in range(chips):
        b = other_chip(i)

        @pl.loop(0, groups)
        def _(u):
            for d in range(1, GROUP):
                second_copy(d, b, peer(u, d)).wait_recv()

        lam_pair(b).start()

    @pl.loop(0, cols)
    def _(j):
        for i in range(chips):
            b = other_chip(i)
            theirs = lax.rem(partner + 2 * i, bins)
            pair_chunk(theirs, j).wait_recv()
            write_chunk(theirs, j).start()

    for i in range(chips):
        lam_pair(other_chip(i)).wait()

    @pl.loop(0, cols)
    def _(j):
        for b in range(bins):
            write_chunk(b, j).wait()
        for i in range(chips):
            pair_chunk(other_chip(i), j).wait_send()
        for i in range(1, chips):
            for q in range(1, PARTS):
                y_copy(i, j, q).wait_send()

    @pl.loop(0, singles + doubles)
    def _(item):
        for d in range(1, GROUP):
            member_copy(item, d, me, col, 0).wait_send()

    @pl.loop(0, doubles)
    def _(s):
        b = lax.rem(me + 2 * lax.rem(s, chips), bins)
        for d in range(1, GROUP):
            second_copy(d, b, peer(s // chips, 0)).wait_send()

    @pl.loop(1, groups)
    def _(u):
        first_copy(0, u).wait_send()

    for i in range(1, chips):
        @pl.loop(0, groups)
        def _(u):
            first_copy(i, u).wait_send()
            curve_copy(i, u).wait_send()

    @pl.loop(1, cols)
    def _(i):
        table_copy(i).wait_send()


def per_device(slope, curvature, target_mean, target_var, table):
    cols = lax.axis_size("col")
    bins = lax.axis_size("bin")
    all_species, pts = table.shape
    rows = all_species // cols
    pad = -(-rows // 8) * 8
    total_pts = pts * cols
    per_shard = slope.shape[0]
    sub = per_shard // cols // LANES
    width = sub * LANES
    chips = bins // 2
    groups = cols // GROUP
    items = groups * (PARTS - 1 + chips)

    def blocks(a):
        return a.reshape(cols, sub, LANES)

    placed = lax.dynamic_update_slice(
        jnp.zeros((cols, pad, LANES), jnp.float32),
        table.reshape(cols, rows, pts),
        (0, 0, lax.axis_index("col") * pts % LANES),
    )
    vmem = pl.BlockSpec(memory_space=pltpu.VMEM)
    hbm = pl.BlockSpec(memory_space=pltpu.HBM)
    dma = pltpu.SemaphoreType.DMA
    species_mean, lam = pl.pallas_call(
        functools.partial(kernel, cols, bins, total_pts, rows),
        out_shape=(
            jax.ShapeDtypeStruct((rows, per_shard * bins), jnp.float32),
            jax.ShapeDtypeStruct((bins, cols, sub, LANES), jnp.float32),
        ),
        in_specs=[hbm] * 4 + [vmem],
        out_specs=(pl.BlockSpec(memory_space=pl.ANY), vmem),
        scratch_shapes=[
            pltpu.VMEM((3, sub, LANES), jnp.float32),
            pltpu.VMEM((bins, cols, sub, LANES), jnp.float32),
            pltpu.VMEM((cols, GROUP, pad, LANES), jnp.float32),
            pltpu.VMEM((2 * GROUP * pad + 16, total_pts), jnp.bfloat16),
            pltpu.VMEM((total_pts, LANES), jnp.float32),
            pltpu.VMEM((items, GROUP, rows, width // PARTS), jnp.float32),
            pltpu.VMEM((bins, cols, rows, width), jnp.float32),
            dma((4,)),
            dma((cols,)), dma((cols,)),
            dma((chips, groups)), dma((chips, cols)),
            dma((chips, groups)), dma((chips, cols)),
            dma((chips, groups, GROUP)), dma((chips, cols)),
            dma((chips,)), dma((chips,)),
            dma((items, GROUP)), dma((chips, cols, PARTS)),
            dma((chips, cols, PARTS)), dma((chips, cols, PARTS)),
            dma((chips, cols)), dma((chips, cols)),
            dma((bins, cols)),
        ],
        compiler_params=pltpu.CompilerParams(collective_id=0, has_side_effects=True, vmem_limit_bytes=40 << 20),
    )(blocks(slope), blocks(curvature), blocks(target_mean), blocks(target_var), placed)
    return species_mean, lam.reshape(-1)


def solution(mesh):
    placed = (P("bin"), P("bin"), P("bin"), P("bin"), P(None, "col"))
    return jax.shard_map(
        per_device, mesh=mesh, in_specs=placed, out_specs=(P("col", None), P()), check_vma=False
    )
```

time: 137 us -> 48.9 us (0.36)
  blocking collectives: 95.4 us -> 0 us
  Pallas kernels: 0 us -> 40.6 us
  between operations: 14.1 us -> 0.67 us
  other arithmetic: 12.6 us -> 0 us
  matrix products: 7.4 us -> 0 us
    all_gather x3 -> x0, blocking collectives: 70.4 us -> none  [the longest x1 32.7 us: per_device(): full_table = lax.all_gather(table, 'col', axis=1, tiled=True)]
    pallas_call x0 -> x1, Pallas kernels: none -> 40.6 us  [per_device(): pl.pallas_call(functools.partial(kernel, cols, bins, total_pts, rows), ou...]
    all_to_all x1 -> x0, blocking collectives: 25 us -> none  [per_device(): lax.all_to_all(terms, 'col', split_axis=0, concat_axis=1, tiled=True)]
    reduce_sum x4 -> x0, other arithmetic: 10.3 us -> none  [the longest x3 8.13 us: per_device(): partition = jnp.sum(expo, axis=0)]
    dot_general x1 -> x0, matrix products: 7.4 us -> none  [per_device(): jnp.dot(full_table, weights, precision=lax.Precision.HIGHEST, preferred_e...]
    add x3 -> x0, other arithmetic: 2.29 us -> none  [per_device(): own_lam = own_lam + (own_mean - moment / partition) / own_var]
    dynamic_slice x2 -> x0, local copies, waits for them, and re-layouts: 1.44 us -> none  [the longest x1 0.72 us: per_device(): own_curve = lax.dynamic_slice_in_dim(curvature, offset, width, 0)]
    unnamed x5 -> x10, local copies, waits for them, and re-layouts: 5.38 us -> 6.45 us
  transfers between devices with their start and end apart: 1 -> 0, of which waited for: 0 -> 0; matrix products, arithmetic and copies ran while one was open for 0% -> 0% of each run, Pallas kernels for 0% -> 0%
where the time goes in v2:
time: 48.9 us; the launch traced here: 48.6 us
  Pallas kernels  40.6 us (83%)
  local copies, waits for them, and re-layouts  7.34 us (15%)
  between operations  0.67 us (1%)
    pallas_call x1, Pallas kernels, per_device(): pl.pallas_call(functools.partial(kernel, cols, bins, total_pts, rows), ou...  40.6 us
    unnamed x10, local copies, waits for them, and re-layouts  6.45 us

profile of v2, /device:TPU:0, one launch (start us, length us, event | category | flops | bytes accessed | tf_op | source)
XLA Modules:
  0.0 48.6 jit_solution(4359378885328188724)
XLA Ops:
  0.7 0.9 %dynamic_update_slice.3.placed_ref = f32[8,8,128]{2,1,0:T(8,128)S(1)} dynamic-update-slice(f32[8,8,128]{2,1,0:T(8,128)S(1)} %broadcast_in_dim.3, f32[8,8,64]{2,1,0:T(8,128)} %bitcast.11, s32[]{:T(128)} %constant.18.clone.1, s32[]{:T(128)} %constant.18.clone.1, s32[]{:T(128)S(6)} %select_n.11) | dynamic-update-slice | bytes 32772 | tf_op jit(solution)/shard_map/dynamic_update_slice | solution.py:388
  1.5 0.0 copy-start
  1.5 0.9 %copy-done = f32[32768]{0:T(1024)S(1)} copy-done((f32[32768]{0:T(1024)S(1)}, f32[32768]{0:T(1024)}, u32[]{:S(2)}) %copy-start) | copy-done | bytes 131096
  2.4 0.0 copy-start.1
  2.5 0.9 %copy-done.1 = f32[32768]{0:T(1024)S(1)} copy-done((f32[32768]{0:T(1024)S(1)}, f32[32768]{0:T(1024)}, u32[]{:S(2)}) %copy-start.1) | copy-done | bytes 131096
  3.4 0.0 copy-start.2
  3.4 0.9 %copy-done.2 = f32[32768]{0:T(1024)S(1)} copy-done((f32[32768]{0:T(1024)S(1)}, f32[32768]{0:T(1024)}, u32[]{:S(2)}) %copy-start.2) | copy-done | bytes 131096
  4.3 0.0 copy-start.3
  4.3 0.9 %copy-done.3 = f32[32768]{0:T(1024)S(1)} copy-done((f32[32768]{0:T(1024)S(1)}, f32[32768]{0:T(1024)}, u32[]{:S(2)}) %copy-start.3) | copy-done | bytes 131096
  5.2 40.6 %shard_map.68 = (f32[8,131072]{1,0:T(8,128)S(1)}, f32[4,8,32,128]{3,2,1,0:T(8,128)S(1)}) custom-call(f32[8,32,128]{2,1,0:T(8,128)S(1)} %bitcast.7, f32[8,32,128]{2,1,0:T(8,128)S(1)} %bitcast.8, f32[8,32,128]{2,1,0:T(8,128)S(1)} %bitcast.9, f32[8,32,128]{2,1,0:T(8,128)S(1)} %bitcast.10, f32[8,8,128]{2,1,0:T(8,128)S(1)} %dynamic_update_slice.3.placed_ref), custom_call_target="tpu_custom_call" | custom-call | tf_op jit(solution)/shard_map/pallas_call | solution.py:396
  45.8 2.0 %copy.10 = f32[8,131072]{1,0:T(8,128)} copy(f32[8,131072]{1,0:T(8,128)S(1)} %get-tuple-element.8) | data formatting | bytes 8388608
  47.8 0.8 %copy.11 = f32[131072]{0:T(1024)} copy(f32[131072]{0:T(1024)S(1)} %bitcast.6) | data formatting | bytes 1048576
  (1 shorter events, 0.0 us)
Async XLA Ops:
  1.5 0.9 %copy-start = (f32[32768]{0:T(1024)S(1)}, f32[32768]{0:T(1024)}, u32[]{:S(2)}) copy-start(f32[32768]{0:T(1024)} %param.5) | copy-start | bytes 393220
  2.4 0.9 %copy-start.1 = (f32[32768]{0:T(1024)S(1)}, f32[32768]{0:T(1024)}, u32[]{:S(2)}) copy-start(f32[32768]{0:T(1024)} %param.6) | copy-start | bytes 393220
  3.4 0.9 %copy-start.2 = (f32[32768]{0:T(1024)S(1)}, f32[32768]{0:T(1024)}, u32[]{:S(2)}) copy-start(f32[32768]{0:T(1024)} %param.7) | copy-start | bytes 393220
  4.3 0.9 %copy-start.3 = (f32[32768]{0:T(1024)S(1)}, f32[32768]{0:T(1024)}, u32[]{:S(2)}) copy-start(f32[32768]{0:T(1024)} %param.8) | copy-start | bytes 393220

commit v3 on v2

--- a/solution.py
+++ b/solution.py
@@ -80,17 +80,26 @@
     var = own[2]
     lam = own[0]
 
+    h = 1.0 / total_pts
+    bend = jnp.exp2(curve2 * (2.0 * h * h))
+
     def newton(lam):
         lam2 = lam * LOG2E
 
         def body(g, carry):
             total, mom = carry
-            for i in range(UNROLL):
-                c = ((g * UNROLL + i).astype(jnp.float32) + 0.5) * (1.0 / total_pts)
-                e = jnp.exp2(c * (lam2 + curve2 * c))
-                total = total + e
-                mom = mom + c * e
-            return total, mom
+            c = ((g * UNROLL).astype(jnp.float32) + 0.5) * h
+            e = jnp.exp2(c * (lam2 + curve2 * c))
+            ratio = jnp.exp2(h * (lam2 + curve2 * (2.0 * c + h)))
+            run = e
+            runs = e
+            for i in range(1, UNROLL):
+                e = e * ratio
+                if i < UNROLL - 1:
+                    ratio = ratio * bend
+                run = run + e
+                runs = runs + run
+            return total + run, mom + (c * run + h * (UNROLL * run - runs))
 
         zero = jnp.zeros_like(lam)
         total, mom = lax.fori_loop(0, total_pts // UNROLL, body, (zero, zero))
@@ -151,14 +160,9 @@
     def _(i):
         table_arrival(i).wait_recv()
 
-    per = LANES // (total_pts // cols)
-    tiles = []
-    for t in range(total_pts // LANES):
-        block = tab[t * per]
-        for n in range(1, per):
-            block = block + tab[t * per + n]
-        tiles.append(block.reshape(GROUP * pad, LANES))
-    full = jnp.concatenate(tiles, axis=1)
+    full = jnp.concatenate(
+        [jnp.concatenate([tab[t, n] for n in range(GROUP)], axis=0) for t in range(cols)], axis=1
+    )
     high = full.astype(jnp.bfloat16).astype(jnp.float32)
     ones = jnp.ones((16, total_pts), jnp.float32)
     lhs[...] = jnp.concatenate([high, full - high, ones], axis=0).astype(jnp.bfloat16)
@@ -373,7 +377,7 @@
     bins = lax.axis_size("bin")
     all_species, pts = table.shape
     rows = all_species // cols
-    pad = -(-rows // 8) * 8
+    pad = rows
     total_pts = pts * cols
     per_shard = slope.shape[0]
     sub = per_shard // cols // LANES
@@ -385,11 +389,7 @@
     def blocks(a):
         return a.reshape(cols, sub, LANES)
 
-    placed = lax.dynamic_update_slice(
-        jnp.zeros((cols, pad, LANES), jnp.float32),
-        table.reshape(cols, rows, pts),
-        (0, 0, lax.axis_index("col") * pts % LANES),
-    )
+    placed = table.reshape(cols, rows, pts)
     vmem = pl.BlockSpec(memory_space=pltpu.VMEM)
     hbm = pl.BlockSpec(memory_space=pltpu.HBM)
     dma = pltpu.SemaphoreType.DMA
@@ -404,7 +404,7 @@
         scratch_shapes=[
             pltpu.VMEM((3, sub, LANES), jnp.float32),
             pltpu.VMEM((bins, cols, sub, LANES), jnp.float32),
-            pltpu.VMEM((cols, GROUP, pad, LANES), jnp.float32),
+            pltpu.VMEM((cols, GROUP, pad, pts), jnp.float32),
             pltpu.VMEM((2 * GROUP * pad + 16, total_pts), jnp.bfloat16),
             pltpu.VMEM((total_pts, LANES), jnp.float32),
             pltpu.VMEM((items, GROUP, rows, width // PARTS), jnp.float32),
@@ -421,7 +421,10 @@
             dma((bins, cols)),
         ],
         compiler_params=pltpu.CompilerParams(collective_id=0, has_side_effects=True, vmem_limit_bytes=40 << 20),
-    )(blocks(slope), blocks(curvature), blocks(target_mean), blocks(target_var), placed)
+    )(*[
+        pltpu.with_memory_space_constraint(a, pltpu.HBM)
+        for a in (blocks(slope), blocks(curvature), blocks(target_mean), blocks(target_var))
+    ], placed)
     return species_mean, lam.reshape(-1)
 
 

time: 48.9 us -> 43.7 us (0.89)
  local copies, waits for them, and re-layouts: 7.34 us -> 3.59 us
  Pallas kernels: 40.6 us -> 39.2 us
    unnamed x10 -> x4, local copies, waits for them, and re-layouts: 6.45 us -> 3.59 us
    pallas_call x1, Pallas kernels: 40.6 us -> 39.2 us  [per_device(): pl.pallas_call(functools.partial(kernel, cols, bins, total_pts, rows), ou...]
    dynamic_update_slice x1 -> x0, local copies, waits for them, and re-layouts: 0.89 us -> none  [per_device(): lax.dynamic_update_slice(jnp.zeros((cols, pad, LANES), jnp.float32), tabl...]
where the time goes in v3:
time: 43.7 us; the launch traced here: 43.5 us
  Pallas kernels  39.2 us (90%)
  local copies, waits for them, and re-layouts  3.59 us (8%)
  between operations  0.65 us (1%)
    pallas_call x1, Pallas kernels, per_device(): pl.pallas_call(functools.partial(kernel, cols, bins, total_pts, rows), ou...  39.2 us
    unnamed x4, local copies, waits for them, and re-layouts  3.59 us

profile of v3, /device:TPU:0, one launch (start us, length us, event | category | flops | bytes accessed | tf_op | source)
XLA Modules:
  0.0 43.5 jit_solution(12136822282123955286)
XLA Ops:
  0.6 0.0 copy-start
  0.6 0.7 %copy-done = f32[64,64]{1,0:T(8,128)S(1)} copy-done((f32[64,64]{1,0:T(8,128)S(1)}, f32[64,64]{1,0:T(8,128)}, u32[]{:S(2)}) %copy-start) | copy-done | bytes 16408
  1.4 39.2 %shard_map.68 = (f32[8,131072]{1,0:T(8,128)S(1)}, f32[4,8,32,128]{3,2,1,0:T(8,128)S(1)}) custom-call(f32[8,32,128]{2,1,0:T(8,128)} %bitcast.8, f32[8,32,128]{2,1,0:T(8,128)} %bitcast.9, f32[8,32,128]{2,1,0:T(8,128)} %bitcast.10, f32[8,32,128]{2,1,0:T(8,128)} %bitcast.11, f32[8,8,64]{2,1,0:T(8,128)S(1)} %bitcast.7), custom_call_target="tpu_custom_call" | custom-call | tf_op jit(solution)/shard_map/pallas_call | solution.py:396
  40.6 2.0 %copy.9 = f32[8,131072]{1,0:T(8,128)} copy(f32[8,131072]{1,0:T(8,128)S(1)} %get-tuple-element.8) | data formatting | bytes 8388608
  42.7 0.8 %copy.10 = f32[131072]{0:T(1024)} copy(f32[131072]{0:T(1024)S(1)} %bitcast.6) | data formatting | bytes 1048576
Async XLA Ops:
  0.6 0.8 %copy-start = (f32[64,64]{1,0:T(8,128)S(1)}, f32[64,64]{1,0:T(8,128)}, u32[]{:S(2)}) copy-start(f32[64,64]{1,0:T(8,128)} %param.9) | copy-start | bytes 49156

commit v4 on v3

--- a/solution.py
+++ b/solution.py
@@ -260,9 +260,9 @@
             member_copy(s, d, me, j, q).start()
         hand_on(me, j, q)
 
-        @pl.when(s > 1)
+        @pl.when(s > 2)
         def _():
-            single_arrivals(s - 2)
+            single_arrivals(s - 3)
 
     for i in range(1, chips):
         @pl.loop(0, groups)
@@ -282,9 +282,9 @@
             member_copy(singles + s, d, b, j, 0).start()
         hand_on(b, j, 0)
 
-        @pl.when(s < 2)
+        @pl.when(s < 3)
         def _():
-            single_arrivals(singles - 2 + s)
+            single_arrivals(singles - 3 + s)
 
     def second_copy(d, b, j):
         to = lax.rem(member + d, GROUP)

time: 43.7 us -> 43.8 us (level)
  no operation moved by 1% of the time
where the time goes in v4:
time: 43.8 us; the launch traced here: 43.5 us
  Pallas kernels  39.3 us (90%)
  local copies, waits for them, and re-layouts  3.59 us (8%)
  between operations  0.65 us (1%)
    pallas_call x1, Pallas kernels, per_device(): pl.pallas_call(functools.partial(kernel, cols, bins, total_pts, rows), ou...  39.3 us
    unnamed x4, local copies, waits for them, and re-layouts  3.59 us

profile of v4, /device:TPU:0, one launch (start us, length us, event | category | flops | bytes accessed | tf_op | source)
XLA Modules:
  0.0 43.5 jit_solution(8837551737281680967)
XLA Ops:
  0.6 0.0 copy-start
  0.6 0.7 %copy-done = f32[64,64]{1,0:T(8,128)S(1)} copy-done((f32[64,64]{1,0:T(8,128)S(1)}, f32[64,64]{1,0:T(8,128)}, u32[]{:S(2)}) %copy-start) | copy-done | bytes 16408
  1.4 39.3 %shard_map.68 = (f32[8,131072]{1,0:T(8,128)S(1)}, f32[4,8,32,128]{3,2,1,0:T(8,128)S(1)}) custom-call(f32[8,32,128]{2,1,0:T(8,128)} %bitcast.8, f32[8,32,128]{2,1,0:T(8,128)} %bitcast.9, f32[8,32,128]{2,1,0:T(8,128)} %bitcast.10, f32[8,32,128]{2,1,0:T(8,128)} %bitcast.11, f32[8,8,64]{2,1,0:T(8,128)S(1)} %bitcast.7), custom_call_target="tpu_custom_call" | custom-call | tf_op jit(solution)/shard_map/pallas_call | solution.py:396
  40.7 2.0 %copy.9 = f32[8,131072]{1,0:T(8,128)} copy(f32[8,131072]{1,0:T(8,128)S(1)} %get-tuple-element.8) | data formatting | bytes 8388608
  42.7 0.8 %copy.10 = f32[131072]{0:T(1024)} copy(f32[131072]{0:T(1024)S(1)} %bitcast.6) | data formatting | bytes 1048576
Async XLA Ops:
  0.6 0.8 %copy-start = (f32[64,64]{1,0:T(8,128)S(1)}, f32[64,64]{1,0:T(8,128)}, u32[]{:S(2)}) copy-start(f32[64,64]{1,0:T(8,128)} %param.9) | copy-start | bytes 49156
